TPU v7x, 32 devices: a whole 2x2x4 slice. The times are simulated.
32 devices in a mesh: lat: 4 (over y, x), lon: 8 (over z, core).
Axes of the slice: x: 2, y: 2, z: 4, core: 2. Of those that a mesh axis runs over, the one named last changes fastest.
Arguments:
- right_side: float32 [8, 768, 1024], P(None, 'lat', 'lon'), may hold values from -16 to 16
- center: float32 [768, 1024], P('lat', 'lon'), may hold values from 3.7 to 5.5
- couplings: float32 [4, 768, 1024], P(None, 'lat', 'lon'), may hold values from 0.15 to 0.45
- land_sea: int32 [768, 1024], P('lat', 'lon'), may hold values 0 or 1
- fold_partner: int32 [1024], replicated, may hold values from 0 to 1023, as said below
Outputs:
- solution: float32 [8, 768, 1024], P(None, 'lat', 'lon')
- residual: float32 [8, 768, 1024], P(None, 'lat', 'lon')
Inputs may be any that keep to these rules, and one draw needn't show every extreme that they name: fold_partner[i] = (s - i) mod 1024 for one integer s, so fold_partner[fold_partner[i]] = i.
All inputs are finite; a program needn't handle non-finite values. No bound on the sum of `land_sea` on one device may be relied on, other than what follows from the above.
Results may differ from a plain program's by a relative error of at most 0.0003.
Values sent between devices are 32-bit elements; how exact they have to be, the bound alone decides.
A program may use at most 64 MiB of HBM per device.

v0:
```python
import jax
import jax.numpy as jnp
from jax import lax
from jax.sharding import PartitionSpec as P

ITERS = 3


def extended(cells, sides, width, closed):
    for axis, dim in sides:
        count = lax.axis_size(axis)
        ends = count if closed else count - 1
        head = lax.slice_in_dim(cells, 0, width, axis=dim)
        tail = lax.slice_in_dim(cells, cells.shape[dim] - width, cells.shape[dim], axis=dim)
        cells = jnp.concatenate(
            [
                lax.ppermute(tail, axis, [(i, (i + 1) % count) for i in range(ends)]),
                cells,
                lax.ppermute(head, axis, [((i + 1) % count, i) for i in range(ends)]),
            ],
            axis=dim,
        )
    return cells


def body(right_side, center, couplings, land_sea, fold_partner):
    row_count, col_count = center.shape
    lat_last = lax.axis_index("lat") == lax.axis_size("lat") - 1
    lat_first = lax.axis_index("lat") == 0
    first_col = lax.axis_index("lon") * col_count
    partner_local = lax.dynamic_slice_in_dim(fold_partner, first_col, col_count, 0)
    ocean_mask = land_sea.astype(jnp.float32)
    north_top = couplings[1, -1, :]
    whole_north = lax.all_gather(north_top, "lon", axis=0, tiled=True)
    fold_coeff = 0.5 * (north_top + jnp.take(whole_north, partner_local, axis=0))
    row_index = lax.broadcasted_iota(jnp.int32, (row_count, col_count), 0)
    top_rows = jnp.logical_and(lat_last, row_index == row_count - 1)
    east_coeff = couplings[0]
    north_coeff = jnp.where(top_rows, fold_coeff[None, :], couplings[1])
    northeast = jnp.where(top_rows, 0.0, couplings[2])
    northwest = jnp.where(top_rows, 0.0, couplings[3])
    stacked = jnp.stack([east_coeff, north_coeff, northeast, northwest])
    coeff_padded = extended(stacked, (("lat", 1), ("lon", 2)), 1, True)
    ghost_rows = lax.broadcasted_iota(jnp.int32, (1, row_count + 2, col_count + 2), 1)
    coeff_padded = jnp.where(jnp.logical_and(lat_first, ghost_rows == 0), 0.0, coeff_padded)
    west_coeff = coeff_padded[0, 1:-1, :-2]
    south_coeff = coeff_padded[1, :-2, 1:-1]
    southwest = coeff_padded[2, :-2, :-2]
    southeast = coeff_padded[3, :-2, 2:]

    def operate(vector):
        top_row = vector[:, -1, :]
        whole_top = lax.all_gather(top_row, "lon", axis=1, tiled=True)
        fold_ghost = jnp.take(whole_top, partner_local, axis=1)
        lon_padded = extended(vector, (("lon", 2),), 1, True)
        padded = extended(lon_padded, (("lat", 1),), 1, False)
        north_row = jnp.where(lat_last, fold_ghost, padded[:, -1, 1:-1])
        padded = padded.at[:, -1, 1:-1].set(north_row)
        upper = padded[:, 2:, 1:-1]
        lower = padded[:, :-2, 1:-1]
        beside = east_coeff * padded[:, 1:-1, 2:] + west_coeff * padded[:, 1:-1, :-2]
        beside = beside + north_coeff * upper + south_coeff * lower
        beside = beside + northeast * padded[:, 2:, 2:] + southwest * padded[:, :-2, :-2]
        beside = beside + northwest * padded[:, 2:, :-2] + southeast * padded[:, :-2, 2:]
        return ocean_mask * (center * vector - beside)

    def paired_sums(residual, scaled, image):
        return lax.psum(
            (jnp.sum(residual * scaled, axis=(1, 2)), jnp.sum(scaled * image, axis=(1, 2))),
            ("lat", "lon"),
        )

    residual = right_side * ocean_mask
    solution = jnp.zeros_like(residual)
    scaled = residual / center
    image = operate(scaled)
    gamma_now, curve = paired_sums(residual, scaled, image)
    step_size = gamma_now / curve
    direction = scaled
    along_dir = image
    for iteration in range(ITERS):
        solution = solution + step_size[:, None, None] * direction
        residual = residual - step_size[:, None, None] * along_dir
        if iteration + 1 < ITERS:
            scaled = residual / center
            image = operate(scaled)
            gamma_next, curve = paired_sums(residual, scaled, image)
            beta_ratio = gamma_next / gamma_now
            step_size = gamma_next / (curve - beta_ratio * gamma_next / step_size)
            direction = scaled + beta_ratio[:, None, None] * direction
            along_dir = image + beta_ratio[:, None, None] * along_dir
            gamma_now = gamma_next
    return (solution, residual)


def solution(mesh):
    return jax.shard_map(
        body,
        mesh=mesh,
        in_specs=(
            P(None, "lat", "lon"),
            P("lat", "lon"),
            P(None, "lat", "lon"),
            P("lat", "lon"),
            P(),
        ),
        out_specs=(P(None, "lat", "lon"), P(None, "lat", "lon")),
        check_vma=False,
    )
```

profile of v0, /device:TPU:0, one launch (start us, length us, event | category | flops | bytes accessed | tf_op | source)
XLA Modules:
  0.0 254.5 jit_solution(16460176406055515500)
XLA Ops:
  1.4 13.4 %all-gather.1 = f32[1,1,1024]{2,1,0:T(1,128)S(1)} all-gather(f32[1,1,128]{2,1,0:T(1,128)S(1)} %slice.247), channel_id=3, replica_groups=mesh['lat'=4,'lon'=8] {'lon'}, dimensions={2}, use_global_device_ids=true | all-gather | bytes 4608 | tf_op jit(solution)/shard_map/all_gather | solution.py:34
  17.3 1.7 slice_select_fusion.2
  19.0 1.5 collective-permute-start.4
  20.6 1.4 collective-permute-start.5
  23.3 1.5 copy.91
  27.7 2.5 collective-permute-start.7
  30.2 13.8 %all-gather = f32[8,1,1024]{2,1,0:T(1,128)S(1)} all-gather(f32[8,1,128]{2,1,0:T(1,128)S(1)} %slice.304), channel_id=2, replica_groups=mesh['lat'=4,'lon'=8] {'lon'}, dimensions={2}, use_global_device_ids=true | all-gather | bytes 36864 | tf_op jit(solution)/shard_map/all_gather | solution.py:53
  45.4 2.4 maximum_select_fusion
  48.5 2.5 collective-permute-start.2
  52.3 2.0 slice_bitcast_fusion.3
  54.3 2.7 %collective-permute-done.3 = f32[8,1,130]{2,0,1:T(8,128)S(1)} collective-permute-done((f32[8,1,130]{2,0,1:T(8,128)S(1)}, f32[8,1,130]{2,0,1:T(8,128)S(1)}, u32[]{:S(2)}, u32[]{:S(2)}) %collective-permute-start.3) | collective-permute-done | bytes 4192 | tf_op jit(solution)/shard_map/ppermute | solution.py:19
  58.2 1.3 scatter.10
  59.6 2.5 multiply_reduce_fusion.4
  62.1 39.8 %all-reduce.2 = (f32[8]{0:T(128)S(1)}, f32[8]{0:T(128)S(1)}) all-reduce(f32[8]{0:T(128)S(1)} %get-tuple-element.50, f32[8]{0:T(128)S(1)} %get-tuple-element.49), channel_id=1, replica_groups=mesh['lat'=4,'lon'=8] {'lat','lon'}, use_global_device_ids=true, to_apply=%region_1.2 | all-reduce | flops 16 | bytes 128 | tf_op jit(solution)/shard_map/psum | solution.py:68
  101.9 2.0 broadcast_divide_fusion.1
  104.9 3.5 %collective-permute-start.9 = (f32[8,192,1]{1,0,2:T(8,128)S(1)}, f32[8,192,1]{1,0,2:T(8,128)S(1)}, u32[]{:S(2)}, u32[]{:S(2)}) collective-permute-start(f32[8,192,1]{1,0,2:T(8,128)S(1)} %copy.100), channel_id=1, source_target_pairs={{1,0},{2,1},{3,2},{4,3},{5,4},{6,5},{7,6},{0,7},{9,8},{10,9},{11,1... | collective-permute-start | bytes 18440 | tf_op jit(solution)/shard_map/ppermute | solution.py:19
  111.6 4.8 %collective-permute-start.10 = (f32[8,1,130]{2,0,1:T(8,128)S(1)}, f32[8,1,130]{2,0,1:T(8,128)S(1)}, u32[]{:S(2)}, u32[]{:S(2)}) collective-permute-start(f32[8,1,130]{2,0,1:T(8,128)S(1)} %copy.103), channel_id=1, source_target_pairs={{0,8},{8,16},{16,24},{1,9},{9,17},{17,25},{2,10},{10,18},{18,26},{... | collective-permute-start | bytes 12488 | tf_op jit(solution)/shard_map/ppermute | solution.py:17
  116.4 9.9 %all-gather.2 = f32[8,1,1024]{2,1,0:T(1,128)S(1)} all-gather(f32[8,1,128]{2,1,0:T(1,128)S(1)} %slice.322), channel_id=4, replica_groups=mesh['lat'=4,'lon'=8] {'lon'}, dimensions={2}, use_global_device_ids=true | all-gather | bytes 36864 | tf_op jit(solution)/shard_map/all_gather | solution.py:53
  127.3 1.7 gather_fusion.2
  129.1 2.1 pad_maximum_fusion
  131.3 1.3 scatter.11
  132.7 3.4 %multiply_reduce_fusion.2 = (f32[8]{0:T(128)S(1)}, f32[8]{0:T(128)S(1)}, f32[8,192,128]{2,1,0:T(8,128)}) fusion(f32[8,192,128]{2,1,0:T(8,128)} %get-tuple-element.71, f32[192,128]{1,0:T(8,128)} %param.14, f32[8,194,130]{2,1,0:T(8,128)S(1)} %scatter.11, f32[192,128]{1,0:T(8,128)} %get-tuple-element.82, f32[192,128]{1,0:T(8,128)S(1)} %bitcast.51, ...), kind=kLoop, calls=%fused_computation.65 | loop fusion | flops 4521968 | bytes 8847424 | tf_op jit(solution)/shard_map/reduce_sum | solution.py:69
  136.0 39.6 %all-reduce.1 = (f32[8]{0:T(128)S(1)}, f32[8]{0:T(128)S(1)}) all-reduce(f32[8]{0:T(128)S(1)} %get-tuple-element.54, f32[8]{0:T(128)S(1)} %get-tuple-element.53), channel_id=1, replica_groups=mesh['lat'=4,'lon'=8] {'lat','lon'}, use_global_device_ids=true, to_apply=%region_5.7 | all-reduce | flops 16 | bytes 128 | tf_op jit(solution)/shard_map/psum | solution.py:68
  176.2 2.8 %broadcast_divide_fusion = (f32[8,192,128]{2,1,0:T(8,128)S(1)}, f32[8,192,128]{2,1,0:T(8,128)}) fusion(f32[192,128]{1,0:T(8,128)} %param.14, f32[8,192,128]{2,1,0:T(8,128)} %get-tuple-element.71, f32[8,192,128]{2,1,0:T(8,128)} %get-tuple-element.69, f32[8,192,128]{2,1,0:T(8,128)} %copy-done.1, f32[8]{0:T(128)S(1)} %get-tuple-element.68, ...), kind=kLoop, calls=%fused_computation.72 | loop fusion | flops 983040 | bytes 4030528 | tf_op jit(solution)/shard_map/div | solution.py:85
  180.0 3.5 %collective-permute-start.13 = (f32[8,192,1]{1,0,2:T(8,128)S(1)}, f32[8,192,1]{1,0,2:T(8,128)S(1)}, u32[]{:S(2)}, u32[]{:S(2)}) collective-permute-start(f32[8,192,1]{1,0,2:T(8,128)S(1)} %copy.110), channel_id=1, source_target_pairs={{1,0},{2,1},{3,2},{4,3},{5,4},{6,5},{7,6},{0,7},{9,8},{10,9},{11,1... | collective-permute-start | bytes 18440 | tf_op jit(solution)/shard_map/ppermute | solution.py:19
  186.7 4.8 %collective-permute-start.14 = (f32[8,1,130]{2,0,1:T(8,128)S(1)}, f32[8,1,130]{2,0,1:T(8,128)S(1)}, u32[]{:S(2)}, u32[]{:S(2)}) collective-permute-start(f32[8,1,130]{2,0,1:T(8,128)S(1)} %copy.113), channel_id=1, source_target_pairs={{0,8},{8,16},{16,24},{1,9},{9,17},{17,25},{2,10},{10,18},{18,26},{... | collective-permute-start | bytes 12488 | tf_op jit(solution)/shard_map/ppermute | solution.py:17
  191.5 9.9 %all-gather.3 = f32[8,1,1024]{2,1,0:T(1,128)S(1)} all-gather(f32[8,1,128]{2,1,0:T(1,128)S(1)} %slice.334), channel_id=5, replica_groups=mesh['lat'=4,'lon'=8] {'lon'}, dimensions={2}, use_global_device_ids=true | all-gather | bytes 36864 | tf_op jit(solution)/shard_map/all_gather | solution.py:53
  202.5 1.7 gather_fusion.3
  204.3 2.1 pad_maximum_fusion.1
  207.9 3.5 %multiply_reduce_fusion = (f32[8]{0:T(128)S(1)}, f32[8]{0:T(128)S(1)}, f32[8,192,128]{2,1,0:T(8,128)}) fusion(f32[8,192,128]{2,1,0:T(8,128)} %get-tuple-element.65, f32[192,128]{1,0:T(8,128)} %param.14, f32[8,194,130]{2,1,0:T(8,128)S(1)} %scatter.14, f32[192,128]{1,0:T(8,128)} %get-tuple-element.82, f32[192,128]{1,0:T(8,128)S(1)} %bitcast.52, ...), kind=kLoop, calls=%fused_computation.61 | loop fusion | flops 4521968 | bytes 8847424 | tf_op jit(solution)/shard_map/reduce_sum | solution.py:69
  211.3 39.4 %all-reduce = (f32[8]{0:T(128)S(1)}, f32[8]{0:T(128)S(1)}) all-reduce(f32[8]{0:T(128)S(1)} %get-tuple-element.52, f32[8]{0:T(128)S(1)} %get-tuple-element.51), channel_id=1, replica_groups=mesh['lat'=4,'lon'=8] {'lat','lon'}, use_global_device_ids=true, to_apply=%region_9.11 | all-reduce | flops 16 | bytes 128 | tf_op jit(solution)/shard_map/psum | solution.py:68
  250.8 3.7 %multiply_subtract_fusion = (f32[8,192,128]{2,1,0:T(8,128)}, f32[8,192,128]{2,1,0:T(8,128)}) fusion(f32[8,192,128]{2,1,0:T(8,128)} %get-tuple-element.65, f32[8,192,128]{2,1,0:T(8,128)} %get-tuple-element.63, f32[8]{0:T(128)S(1)} %get-tuple-element.62, f32[8]{0:T(128)S(1)} %get-tuple-element.61, f32[8,192,128]{2,1,0:T(8,128)} %get-tuple-element.69, ...), kind=kLoop, calls=%fused_computation.59 | loop fusion | flops 3735552 | bytes 6488224 | tf_op jit(solution)/shard_map/sub | solution.py:83
  (122 shorter events, 24.5 us)
Async XLA Ops:
  0.6 21.4 %copy-start.9 = (s32[192,128]{1,0:T(8,128)S(1)}, s32[192,128]{1,0:T(8,128)}, u32[]{:S(2)}) copy-start(s32[192,128]{1,0:T(8,128)} %param.16) | copy-start | bytes 294916
  0.6 21.4 %copy-start.8 = (f32[192,128]{1,0:T(8,128)S(1)}, f32[192,128]{1,0:T(8,128)}, u32[]{:S(2)}) copy-start(f32[192,128]{1,0:T(8,128)} %param.14) | copy-start | bytes 294916
  0.7 21.4 %copy-start = (f32[8,192,128]{2,1,0:T(8,128)S(1)}, f32[8,192,128]{2,1,0:T(8,128)}, u32[]{:S(2)}) copy-start(f32[8,192,128]{2,1,0:T(8,128)} %param.13) | copy-start | bytes 2359300
  19.0 26.3 %copy-start.7 = (f32[1,192,128]{2,1,0:T(8,128)}, f32[1,192,128]{2,1,0:T(8,128)S(1)}, u32[]{:S(2)}) copy-start(f32[1,192,128]{2,1,0:T(8,128)S(1)} %get-tuple-element.97) | copy-start | bytes 294916
  19.0 6.6 %collective-permute-start.4 = (f32[4,1,128]{2,1,0:T(1,128)S(1)}, f32[4,1,128]{2,1,0:T(1,128)S(1)}, u32[]{:S(2)}, u32[]{:S(2)}) collective-permute-start(f32[4,1,128]{2,1,0:T(1,128)S(1)} %get-tuple-element.99), channel_id=1, source_target_pairs={{0,8},{8,16},{16,24},{24,0},{1,9},{9,17},{17,25},{25,1},{2,10},{10... | collective-permute-start | bytes 6152 | tf_op jit(solution)/shard_map/ppermute | solution.py:17
  20.6 5.0 %collective-permute-start.5 = (f32[4,1,128]{2,1,0:T(1,128)S(1)}, f32[4,1,128]{2,1,0:T(1,128)S(1)}, u32[]{:S(2)}, u32[]{:S(2)}) collective-permute-start(f32[4,1,128]{2,1,0:T(1,128)S(1)} %get-tuple-element.100), channel_id=1, source_target_pairs={{8,0},{16,8},{24,16},{0,24},{9,1},{17,9},{25,17},{1,25},{10,2},{18... | collective-permute-start | bytes 6152 | tf_op jit(solution)/shard_map/ppermute | solution.py:19
  24.7 23.4 %collective-permute-start.1 = (f32[8,192,1]{1,0,2:T(8,128)S(1)}, f32[8,192,1]{1,0,2:T(8,128)S(1)}, u32[]{:S(2)}, u32[]{:S(2)}) collective-permute-start(f32[8,192,1]{1,0,2:T(8,128)S(1)} %copy.91), channel_id=1, source_target_pairs={{1,0},{2,1},{3,2},{4,3},{5,4},{6,5},{7,6},{0,7},{9,8},{10,9},{11,1... | collective-permute-start | bytes 18440 | tf_op jit(solution)/shard_map/ppermute | solution.py:19
  25.1 22.7 %collective-permute-start = (f32[8,192,1]{1,0,2:T(8,128)S(1)}, f32[8,192,1]{1,0,2:T(8,128)S(1)}, u32[]{:S(2)}, u32[]{:S(2)}) collective-permute-start(f32[8,192,1]{1,0,2:T(8,128)S(1)} %copy.90), channel_id=1, source_target_pairs={{0,1},{1,2},{2,3},{3,4},{4,5},{5,6},{6,7},{7,0},{8,9},{9,10},{10,1... | collective-permute-start | bytes 18440 | tf_op jit(solution)/shard_map/ppermute | solution.py:17
  26.7 18.7 %collective-permute-start.6 = (f32[4,194,1]{2,1,0:T(8,128)}, f32[4,194,1]{2,1,0:T(8,128)S(1)}, u32[]{:S(2)}, u32[]{:S(2)}) collective-permute-start(f32[4,194,1]{2,1,0:T(8,128)} %get-tuple-element.93), channel_id=1, source_target_pairs={{0,1},{1,2},{2,3},{3,4},{4,5},{5,6},{6,7},{7,0},{8,9},{9,10},{10,1... | collective-permute-start | bytes 9320 | tf_op jit(solution)/shard_map/ppermute | solution.py:17
  27.7 17.6 %collective-permute-start.7 = (f32[4,194,1]{2,1,0:T(8,128)}, f32[4,194,1]{2,1,0:T(8,128)}, u32[]{:S(2)}, u32[]{:S(2)}) collective-permute-start(f32[4,194,1]{2,1,0:T(8,128)} %get-tuple-element.94), channel_id=1, source_target_pairs={{1,0},{2,1},{3,2},{4,3},{5,4},{6,5},{7,6},{0,7},{9,8},{10,9},{11,1... | collective-permute-start | bytes 9320 | tf_op jit(solution)/shard_map/ppermute | solution.py:19
  48.5 5.8 %collective-permute-start.2 = (f32[8,1,130]{2,0,1:T(8,128)S(1)}, f32[8,1,130]{2,0,1:T(8,128)S(1)}, u32[]{:S(2)}, u32[]{:S(2)}) collective-permute-start(f32[8,1,130]{2,0,1:T(8,128)S(1)} %get-tuple-element.79), channel_id=1, source_target_pairs={{0,8},{8,16},{16,24},{1,9},{9,17},{17,25},{2,10},{10,18},{18,26},{... | collective-permute-start | bytes 12488 | tf_op jit(solution)/shard_map/ppermute | solution.py:17
  51.0 5.9 %collective-permute-start.3 = (f32[8,1,130]{2,0,1:T(8,128)S(1)}, f32[8,1,130]{2,0,1:T(8,128)S(1)}, u32[]{:S(2)}, u32[]{:S(2)}) collective-permute-start(f32[8,1,130]{2,0,1:T(8,128)S(1)} %get-tuple-element.80), channel_id=1, source_target_pairs={{8,0},{16,8},{24,16},{9,1},{17,9},{25,17},{10,2},{18,10},{26,18},{... | collective-permute-start | bytes 12488 | tf_op jit(solution)/shard_map/ppermute | solution.py:19
  62.1 41.8 %copy-start.1 = (f32[8,192,128]{2,1,0:T(8,128)}, f32[8,192,128]{2,1,0:T(8,128)S(1)}, u32[]{:S(2)}) copy-start(f32[8,192,128]{2,1,0:T(8,128)S(1)} %get-tuple-element.72) | copy-start | bytes 2359300
  104.5 4.9 %collective-permute-start.8 = (f32[8,192,1]{1,0,2:T(8,128)S(1)}, f32[8,192,1]{1,0,2:T(8,128)S(1)}, u32[]{:S(2)}, u32[]{:S(2)}) collective-permute-start(f32[8,192,1]{1,0,2:T(8,128)S(1)} %copy.99), channel_id=1, source_target_pairs={{0,1},{1,2},{2,3},{3,4},{4,5},{5,6},{6,7},{7,0},{8,9},{9,10},{10,1... | collective-permute-start | bytes 18440 | tf_op jit(solution)/shard_map/ppermute | solution.py:17
  104.9 4.9 %collective-permute-start.9 = (f32[8,192,1]{1,0,2:T(8,128)S(1)}, f32[8,192,1]{1,0,2:T(8,128)S(1)}, u32[]{:S(2)}, u32[]{:S(2)}) collective-permute-start(f32[8,192,1]{1,0,2:T(8,128)S(1)} %copy.100), channel_id=1, source_target_pairs={{1,0},{2,1},{3,2},{4,3},{5,4},{6,5},{7,6},{0,7},{9,8},{10,9},{11,1... | collective-permute-start | bytes 18440 | tf_op jit(solution)/shard_map/ppermute | solution.py:19
  109.7 17.6 %copy-start.4 = (f32[8,192,1]{2,1,0:T(8,128)}, f32[8,192,1]{2,1,0:T(8,128)S(1)}, u32[]{:S(2)}) copy-start(f32[8,192,1]{2,1,0:T(8,128)S(1)} %copy.101) | copy-start | bytes 18436
  110.1 19.0 %copy-start.6 = (f32[8,192,1]{2,1,0:T(8,128)}, f32[8,192,1]{2,1,0:T(8,128)S(1)}, u32[]{:S(2)}) copy-start(f32[8,192,1]{2,1,0:T(8,128)S(1)} %copy.102) | copy-start | bytes 18436
  110.3 18.8 %collective-permute-start.11 = (f32[8,1,130]{2,0,1:T(8,128)S(1)}, f32[8,1,130]{2,0,1:T(8,128)S(1)}, u32[]{:S(2)}, u32[]{:S(2)}) collective-permute-start(f32[8,1,130]{2,0,1:T(8,128)S(1)} %copy.123), channel_id=1, source_target_pairs={{8,0},{16,8},{24,16},{9,1},{17,9},{25,17},{10,2},{18,10},{26,18},{... | collective-permute-start | bytes 12488 | tf_op jit(solution)/shard_map/ppermute | solution.py:19
  111.6 17.5 %collective-permute-start.10 = (f32[8,1,130]{2,0,1:T(8,128)S(1)}, f32[8,1,130]{2,0,1:T(8,128)S(1)}, u32[]{:S(2)}, u32[]{:S(2)}) collective-permute-start(f32[8,1,130]{2,0,1:T(8,128)S(1)} %copy.103), channel_id=1, source_target_pairs={{0,8},{8,16},{16,24},{1,9},{9,17},{17,25},{2,10},{10,18},{18,26},{... | collective-permute-start | bytes 12488 | tf_op jit(solution)/shard_map/ppermute | solution.py:17
  132.6 43.0 %copy-start.18 = (f32[8]{0:T(128)S(1)}, f32[8]{0:T(128)}, u32[]{:S(2)}) copy-start(f32[8]{0:T(128)} %copy-done.17) | copy-start | bytes 100
  132.7 43.0 %copy-start.20 = (f32[8]{0:T(128)S(1)}, f32[8]{0:T(128)}, u32[]{:S(2)}) copy-start(f32[8]{0:T(128)} %copy-done.19) | copy-start | bytes 100
  179.7 4.9 %collective-permute-start.12 = (f32[8,192,1]{1,0,2:T(8,128)S(1)}, f32[8,192,1]{1,0,2:T(8,128)S(1)}, u32[]{:S(2)}, u32[]{:S(2)}) collective-permute-start(f32[8,192,1]{1,0,2:T(8,128)S(1)} %copy.109), channel_id=1, source_target_pairs={{0,1},{1,2},{2,3},{3,4},{4,5},{5,6},{6,7},{7,0},{8,9},{9,10},{10,1... | collective-permute-start | bytes 18440 | tf_op jit(solution)/shard_map/ppermute | solution.py:17
  180.0 4.9 %collective-permute-start.13 = (f32[8,192,1]{1,0,2:T(8,128)S(1)}, f32[8,192,1]{1,0,2:T(8,128)S(1)}, u32[]{:S(2)}, u32[]{:S(2)}) collective-permute-start(f32[8,192,1]{1,0,2:T(8,128)S(1)} %copy.110), channel_id=1, source_target_pairs={{1,0},{2,1},{3,2},{4,3},{5,4},{6,5},{7,6},{0,7},{9,8},{10,9},{11,1... | collective-permute-start | bytes 18440 | tf_op jit(solution)/shard_map/ppermute | solution.py:19
  184.9 17.6 %copy-start.3 = (f32[8,192,1]{2,1,0:T(8,128)}, f32[8,192,1]{2,1,0:T(8,128)S(1)}, u32[]{:S(2)}) copy-start(f32[8,192,1]{2,1,0:T(8,128)S(1)} %copy.111) | copy-start | bytes 18436
  185.3 19.0 %copy-start.5 = (f32[8,192,1]{2,1,0:T(8,128)}, f32[8,192,1]{2,1,0:T(8,128)S(1)}, u32[]{:S(2)}) copy-start(f32[8,192,1]{2,1,0:T(8,128)S(1)} %copy.112) | copy-start | bytes 18436
  185.4 18.8 %collective-permute-start.15 = (f32[8,1,130]{2,0,1:T(8,128)S(1)}, f32[8,1,130]{2,0,1:T(8,128)S(1)}, u32[]{:S(2)}, u32[]{:S(2)}) collective-permute-start(f32[8,1,130]{2,0,1:T(8,128)S(1)} %copy.124), channel_id=1, source_target_pairs={{8,0},{16,8},{24,16},{9,1},{17,9},{25,17},{10,2},{18,10},{26,18},{... | collective-permute-start | bytes 12488 | tf_op jit(solution)/shard_map/ppermute | solution.py:19
  186.7 17.6 %collective-permute-start.14 = (f32[8,1,130]{2,0,1:T(8,128)S(1)}, f32[8,1,130]{2,0,1:T(8,128)S(1)}, u32[]{:S(2)}, u32[]{:S(2)}) collective-permute-start(f32[8,1,130]{2,0,1:T(8,128)S(1)} %copy.113), channel_id=1, source_target_pairs={{0,8},{8,16},{16,24},{1,9},{9,17},{17,25},{2,10},{10,18},{18,26},{... | collective-permute-start | bytes 12488 | tf_op jit(solution)/shard_map/ppermute | solution.py:17
  207.8 42.9 %copy-start.13 = (f32[8]{0:T(128)S(1)}, f32[8]{0:T(128)}, u32[]{:S(2)}) copy-start(f32[8]{0:T(128)} %copy-done.12) | copy-start | bytes 100
  207.8 42.9 %copy-start.14 = (f32[8]{0:T(128)S(1)}, f32[8]{0:T(128)}, u32[]{:S(2)}) copy-start(f32[8]{0:T(128)} %get-tuple-element.67) | copy-start | bytes 100
  207.8 42.9 %copy-start.2 = (f32[8,192,128]{2,1,0:T(8,128)S(1)}, f32[8,192,128]{2,1,0:T(8,128)}, u32[]{:S(2)}) copy-start(f32[8,192,128]{2,1,0:T(8,128)} %copy-done.1) | copy-start | bytes 2359300
  207.9 42.9 %copy-start.11 = (f32[8]{0:T(128)S(1)}, f32[8]{0:T(128)}, u32[]{:S(2)}) copy-start(f32[8]{0:T(128)} %copy-done.10) | copy-start | bytes 100
  207.9 42.9 %copy-start.16 = (f32[8]{0:T(128)S(1)}, f32[8]{0:T(128)}, u32[]{:S(2)}) copy-start(f32[8]{0:T(128)} %copy-done.15) | copy-start | bytes 100
  (5 other events, 12.3 us)
where the time goes:
time: 255 us; the launch traced here: 254 us
  blocking collectives  166 us (65%)
  starting transfers between devices  30.2 us (12%)
  other arithmetic  29.4 us (12%)
  local copies, waits for them, and re-layouts  23 us (9%)
  waiting for transfers between devices  4.77 us (2%)
    psum x3, blocking collectives, paired_sums(): lax.psum((jnp.sum(residual * scaled, axis=(1, 2)), jnp.sum(scaled * image...  119 us
    all_gather x3, blocking collectives, operate(): whole_top = lax.all_gather(top_row, 'lon', axis=1, tiled=True)  33.6 us
    ppermute x8, starting transfers between devices, extended(): lax.ppermute(tail, axis, [(i, (i + 1) % count) for i in range(ends)])  15.2 us
    ppermute x8, starting transfers between devices, extended(): lax.ppermute(head, axis, [((i + 1) % count, i) for i in range(ends)])  15 us
    all_gather x1, blocking collectives, body(): whole_north = lax.all_gather(north_top, 'lon', axis=0, tiled=True)  13.4 us
    reduce_sum x3, other arithmetic, paired_sums(): jnp.sum(scaled * image, axis=(1, 2))  9.31 us
  transfers between devices with their start and end apart: 16, of which 4 were waited for; matrix products, arithmetic and copies ran while one was open for 7% of the time, Pallas kernels for 0%

commit v1 on v0

--- a/solution.py
+++ b/solution.py
@@ -1,9 +1,18 @@
+import functools
 import jax
 import jax.numpy as jnp
 from jax import lax
 from jax.sharding import PartitionSpec as P
 
 ITERS = 3
+
+
+def _balance_loops(mine, peer_axis, bus_axis):
+    z2 = jax.lax.psum(mine, peer_axis)
+    return jax.lax.psum(z2, bus_axis)
+
+
+detail_the_wall = functools.partial(_balance_loops, peer_axis="lon", bus_axis="lat")
 
 
 def extended(cells, sides, width, closed):
@@ -65,9 +74,8 @@
         return ocean_mask * (center * vector - beside)
 
     def paired_sums(residual, scaled, image):
-        return lax.psum(
-            (jnp.sum(residual * scaled, axis=(1, 2)), jnp.sum(scaled * image, axis=(1, 2))),
-            ("lat", "lon"),
+        return detail_the_wall(
+            (jnp.sum(residual * scaled, axis=(1, 2)), jnp.sum(scaled * image, axis=(1, 2)))
         )
 
     residual = right_side * ocean_mask

time: 255 us -> 206 us (0.81)
  blocking collectives: 166 us -> 117 us
    psum x3 -> x6, blocking collectives: 119 us -> 70.8 us  [the longest x3 42.4 us: _balance_loops(): z2 = jax.lax.psum(mine, peer_axis)]
  transfers between devices with their start and end apart: 16 -> 16, of which waited for: 4 -> 5; matrix products, arithmetic and copies ran while one was open for 7% -> 8% of each run, Pallas kernels for 0% -> 0%
where the time goes in v1:
time: 206 us; the launch traced here: 205 us
  blocking collectives  117 us (57%)
  starting transfers between devices  29.7 us (14%)
  other arithmetic  29.4 us (14%)
  local copies, waits for them, and re-layouts  23 us (11%)
  waiting for transfers between devices  4.78 us (2%)
    psum x3, blocking collectives, _balance_loops(): z2 = jax.lax.psum(mine, peer_axis)  42.4 us
    all_gather x3, blocking collectives, operate(): whole_top = lax.all_gather(top_row, 'lon', axis=1, tiled=True)  33.1 us
    psum x3, blocking collectives, _balance_loops(): return jax.lax.psum(z2, bus_axis)  28.4 us
    ppermute x8, starting transfers between devices, extended(): lax.ppermute(head, axis, [((i + 1) % count, i) for i in range(ends)])  15 us
    ppermute x8, starting transfers between devices, extended(): lax.ppermute(tail, axis, [(i, (i + 1) % count) for i in range(ends)])  14.7 us
    all_gather x1, blocking collectives, body(): whole_north = lax.all_gather(north_top, 'lon', axis=0, tiled=True)  13.4 us
    reduce_sum x3, other arithmetic, paired_sums(): jnp.sum(scaled * image, axis=(1, 2))  9.27 us
    div x3, other arithmetic, body(): scaled = residual / center  4.92 us
  transfers between devices with their start and end apart: 16, of which 5 were waited for; matrix products, arithmetic and copies ran while one was open for 8% of the time, Pallas kernels for 0%

profile of v1, /device:TPU:0, one launch (start us, length us, event | category | flops | bytes accessed | tf_op | source)
XLA Modules:
  0.0 205.3 jit_solution(8067492327026669636)
XLA Ops:
  1.4 13.4 %all-gather.1 = f32[1,1,1024]{2,1,0:T(1,128)S(1)} all-gather(f32[1,1,128]{2,1,0:T(1,128)S(1)} %slice.247), channel_id=3, replica_groups=mesh['lat'=4,'lon'=8] {'lon'}, dimensions={2}, use_global_device_ids=true | all-gather | bytes 4608 | tf_op jit(solution)/shard_map/all_gather | solution.py:43
  17.3 1.7 slice_select_fusion.2
  19.0 1.5 collective-permute-start.4
  23.2 1.5 copy.91
  27.7 2.5 %collective-permute-start.7 = (f32[4,194,1]{2,1,0:T(8,128)}, f32[4,194,1]{2,1,0:T(8,128)}, u32[]{:S(2)}, u32[]{:S(2)}) collective-permute-start(f32[4,194,1]{2,1,0:T(8,128)} %get-tuple-element.100), channel_id=1, source_target_pairs={{1,0},{2,1},{3,2},{4,3},{5,4},{6,5},{7,6},{0,7},{9,8},{10,9},{11,1... | collective-permute-start | bytes 9320 | tf_op jit(solution)/shard_map/ppermute | solution.py:28
  30.2 13.8 %all-gather = f32[8,1,1024]{2,1,0:T(1,128)S(1)} all-gather(f32[8,1,128]{2,1,0:T(1,128)S(1)} %slice.304), channel_id=2, replica_groups=mesh['lat'=4,'lon'=8] {'lon'}, dimensions={2}, use_global_device_ids=true | all-gather | bytes 36864 | tf_op jit(solution)/shard_map/all_gather | solution.py:62
  45.4 2.3 %maximum_select_fusion = f32[4,194,130]{2,1,0:T(8,128)} fusion(f32[4,194,1]{2,1,0:T(8,128)} %collective-permute-done.7, f32[4,1,128]{2,1,0:T(1,128)S(1)} %collective-permute-done.5, f32[1,192,128]{2,1,0:T(8,128)S(1)} %get-tuple-element.102, f32[1,192,128]{2,1,0:T(8,128)S(1)} %get-tuple-element.103, f32[1,192,128]{2,1,0:T(8,128)S(1)} %get-tuple-element.101, ...), kind=kLoop, calls=%fused_computation.7 | loop fusion | flops 807040 | bytes 807234 | tf_op jit(solution)/shard_map/jit(_where)/select_n | solution.py:54
  48.5 2.5 %collective-permute-start.2 = (f32[8,1,130]{2,0,1:T(8,128)S(1)}, f32[8,1,130]{2,0,1:T(8,128)S(1)}, u32[]{:S(2)}, u32[]{:S(2)}) collective-permute-start(f32[8,1,130]{2,0,1:T(8,128)S(1)} %get-tuple-element.85), channel_id=1, source_target_pairs={{0,8},{8,16},{16,24},{1,9},{9,17},{17,25},{2,10},{10,18},{18,26},{... | collective-permute-start | bytes 12488 | tf_op jit(solution)/shard_map/ppermute | solution.py:26
  52.3 1.9 slice_bitcast_fusion.3
  54.3 2.7 %collective-permute-done.3 = f32[8,1,130]{2,0,1:T(8,128)S(1)} collective-permute-done((f32[8,1,130]{2,0,1:T(8,128)S(1)}, f32[8,1,130]{2,0,1:T(8,128)S(1)}, u32[]{:S(2)}, u32[]{:S(2)}) %collective-permute-start.3) | collective-permute-done | bytes 4192 | tf_op jit(solution)/shard_map/ppermute | solution.py:28
  59.6 2.5 %multiply_reduce_fusion.4 = (f32[8]{0:T(128)S(1)}, f32[8]{0:T(128)S(1)}, f32[8,192,128]{2,1,0:T(8,128)S(1)}) fusion(f32[192,128]{1,0:T(8,128)} %param.14, f32[8,192,128]{2,1,0:T(8,128)S(1)} %copy-done, f32[192,128]{1,0:T(8,128)S(1)} %convert_element_type.3, f32[8,194,130]{2,1,0:T(8,128)S(1)} %scatter.10, f32[192,128]{1,0:T(8,128)} %get-tuple-element.88, ...), kind=kLoop, calls=%fused_computation.68 | loop fusion | flops 4718576 | bytes 8847424 | tf_op jit(solution)/shard_map/reduce_sum | solution.py:78
  62.1 13.6 %all-reduce.2 = (f32[8]{0:T(128)S(1)}, f32[8]{0:T(128)S(1)}) all-reduce(f32[8]{0:T(128)S(1)} %get-tuple-element.50, f32[8]{0:T(128)S(1)} %get-tuple-element.49), channel_id=1, replica_groups=mesh['lat'=4,'lon'=8] {'lon'}, use_global_device_ids=true, to_apply=%region_1.2 | all-reduce | flops 16 | bytes 128 | tf_op jit(solution)/shard_map/psum | solution.py:11
  75.7 10.4 %all-reduce.5 = (f32[8]{0:T(128)S(1)}, f32[8]{0:T(128)S(1)}) all-reduce(f32[8]{0:T(128)S(1)} %get-tuple-element.59, f32[8]{0:T(128)S(1)} %get-tuple-element.60), channel_id=1, replica_groups=mesh['lat'=4,'lon'=8] {'lat'}, use_global_device_ids=true, to_apply=%region_2.3 | all-reduce | flops 16 | bytes 128 | tf_op jit(solution)/shard_map/psum | solution.py:12
  86.1 2.0 broadcast_divide_fusion.1
  89.1 3.5 %collective-permute-start.9 = (f32[8,192,1]{1,0,2:T(8,128)S(1)}, f32[8,192,1]{1,0,2:T(8,128)S(1)}, u32[]{:S(2)}, u32[]{:S(2)}) collective-permute-start(f32[8,192,1]{1,0,2:T(8,128)S(1)} %copy.100), channel_id=1, source_target_pairs={{1,0},{2,1},{3,2},{4,3},{5,4},{6,5},{7,6},{0,7},{9,8},{10,9},{11,1... | collective-permute-start | bytes 18440 | tf_op jit(solution)/shard_map/ppermute | solution.py:28
  95.8 4.5 %collective-permute-start.10 = (f32[8,1,130]{2,0,1:T(8,128)S(1)}, f32[8,1,130]{2,0,1:T(8,128)S(1)}, u32[]{:S(2)}, u32[]{:S(2)}) collective-permute-start(f32[8,1,130]{2,0,1:T(8,128)S(1)} %copy.103), channel_id=1, source_target_pairs={{0,8},{8,16},{16,24},{1,9},{9,17},{17,25},{2,10},{10,18},{18,26},{... | collective-permute-start | bytes 12488 | tf_op jit(solution)/shard_map/ppermute | solution.py:26
  100.3 9.7 %all-gather.2 = f32[8,1,1024]{2,1,0:T(1,128)S(1)} all-gather(f32[8,1,128]{2,1,0:T(1,128)S(1)} %slice.322), channel_id=4, replica_groups=mesh['lat'=4,'lon'=8] {'lon'}, dimensions={2}, use_global_device_ids=true | all-gather | bytes 36864 | tf_op jit(solution)/shard_map/all_gather | solution.py:62
  111.0 1.7 gather_fusion.2
  112.8 2.1 %pad_maximum_fusion = f32[8,194,130]{2,1,0:T(8,128)S(1)} fusion(f32[8,1,130]{2,1,0:T(1,128)S(1)} %copy.106, f32[8,192,1]{2,1,0:T(8,128)} %copy-done.6, f32[8,192,128]{2,1,0:T(8,128)S(1)} %get-tuple-element.76, f32[8,192,1]{2,1,0:T(8,128)} %copy-done.4, f32[8,1,130]{2,1,0:T(1,128)S(1)} %copy.105), kind=kLoop, calls=%fused_computation.4 | loop fusion | flops 807040 | bytes 1614080 | tf_op jit(solution)/shard_map/concatenate | solution.py:24
  116.3 3.4 %multiply_reduce_fusion.2 = (f32[8]{0:T(128)S(1)}, f32[8]{0:T(128)S(1)}, f32[8,192,128]{2,1,0:T(8,128)}) fusion(f32[8,192,128]{2,1,0:T(8,128)} %get-tuple-element.77, f32[192,128]{1,0:T(8,128)} %param.14, f32[8,194,130]{2,1,0:T(8,128)S(1)} %scatter.11, f32[192,128]{1,0:T(8,128)} %get-tuple-element.88, f32[192,128]{1,0:T(8,128)S(1)} %bitcast.51, ...), kind=kLoop, calls=%fused_computation.65 | loop fusion | flops 4521968 | bytes 8847424 | tf_op jit(solution)/shard_map/reduce_sum | solution.py:78
  119.7 14.4 %all-reduce.1 = (f32[8]{0:T(128)S(1)}, f32[8]{0:T(128)S(1)}) all-reduce(f32[8]{0:T(128)S(1)} %get-tuple-element.54, f32[8]{0:T(128)S(1)} %get-tuple-element.53), channel_id=1, replica_groups=mesh['lat'=4,'lon'=8] {'lon'}, use_global_device_ids=true, to_apply=%region_7.9 | all-reduce | flops 16 | bytes 128 | tf_op jit(solution)/shard_map/psum | solution.py:11
  134.1 8.5 %all-reduce.4 = (f32[8]{0:T(128)S(1)}, f32[8]{0:T(128)S(1)}) all-reduce(f32[8]{0:T(128)S(1)} %get-tuple-element.57, f32[8]{0:T(128)S(1)} %get-tuple-element.58), channel_id=1, replica_groups=mesh['lat'=4,'lon'=8] {'lat'}, use_global_device_ids=true, to_apply=%region_8.10 | all-reduce | flops 16 | bytes 128 | tf_op jit(solution)/shard_map/psum | solution.py:12
  143.2 2.9 %broadcast_divide_fusion = (f32[8,192,128]{2,1,0:T(8,128)S(1)}, f32[8,192,128]{2,1,0:T(8,128)}) fusion(f32[192,128]{1,0:T(8,128)} %param.14, f32[8,192,128]{2,1,0:T(8,128)} %get-tuple-element.77, f32[8,192,128]{2,1,0:T(8,128)} %get-tuple-element.75, f32[8,192,128]{2,1,0:T(8,128)} %copy-done.1, f32[8]{0:T(128)S(1)} %get-tuple-element.74, ...), kind=kLoop, calls=%fused_computation.72 | loop fusion | flops 983040 | bytes 4030528 | tf_op jit(solution)/shard_map/div | solution.py:93
  147.0 3.5 %collective-permute-start.13 = (f32[8,192,1]{1,0,2:T(8,128)S(1)}, f32[8,192,1]{1,0,2:T(8,128)S(1)}, u32[]{:S(2)}, u32[]{:S(2)}) collective-permute-start(f32[8,192,1]{1,0,2:T(8,128)S(1)} %copy.110), channel_id=1, source_target_pairs={{1,0},{2,1},{3,2},{4,3},{5,4},{6,5},{7,6},{0,7},{9,8},{10,9},{11,1... | collective-permute-start | bytes 18440 | tf_op jit(solution)/shard_map/ppermute | solution.py:28
  153.7 4.5 %collective-permute-start.14 = (f32[8,1,130]{2,0,1:T(8,128)S(1)}, f32[8,1,130]{2,0,1:T(8,128)S(1)}, u32[]{:S(2)}, u32[]{:S(2)}) collective-permute-start(f32[8,1,130]{2,0,1:T(8,128)S(1)} %copy.113), channel_id=1, source_target_pairs={{0,8},{8,16},{16,24},{1,9},{9,17},{17,25},{2,10},{10,18},{18,26},{... | collective-permute-start | bytes 12488 | tf_op jit(solution)/shard_map/ppermute | solution.py:26
  158.2 9.7 %all-gather.3 = f32[8,1,1024]{2,1,0:T(1,128)S(1)} all-gather(f32[8,1,128]{2,1,0:T(1,128)S(1)} %slice.334), channel_id=5, replica_groups=mesh['lat'=4,'lon'=8] {'lon'}, dimensions={2}, use_global_device_ids=true | all-gather | bytes 36864 | tf_op jit(solution)/shard_map/all_gather | solution.py:62
  168.9 1.7 gather_fusion.3
  170.7 2.1 %pad_maximum_fusion.1 = f32[8,194,130]{2,1,0:T(8,128)S(1)} fusion(f32[8,1,130]{2,1,0:T(1,128)S(1)} %copy.116, f32[8,192,1]{2,1,0:T(8,128)} %copy-done.5, f32[8,192,128]{2,1,0:T(8,128)S(1)} %get-tuple-element.70, f32[8,192,1]{2,1,0:T(8,128)} %copy-done.3, f32[8,1,130]{2,1,0:T(1,128)S(1)} %copy.115), kind=kLoop, calls=%fused_computation.5 | loop fusion | flops 807040 | bytes 1614080 | tf_op jit(solution)/shard_map/concatenate | solution.py:24
  174.3 3.4 %multiply_reduce_fusion = (f32[8]{0:T(128)S(1)}, f32[8]{0:T(128)S(1)}, f32[8,192,128]{2,1,0:T(8,128)}) fusion(f32[8,192,128]{2,1,0:T(8,128)} %get-tuple-element.71, f32[192,128]{1,0:T(8,128)} %param.14, f32[8,194,130]{2,1,0:T(8,128)S(1)} %scatter.14, f32[192,128]{1,0:T(8,128)} %get-tuple-element.88, f32[192,128]{1,0:T(8,128)S(1)} %bitcast.52, ...), kind=kLoop, calls=%fused_computation.61 | loop fusion | flops 4521968 | bytes 8847424 | tf_op jit(solution)/shard_map/reduce_sum | solution.py:78
  177.7 14.4 %all-reduce = (f32[8]{0:T(128)S(1)}, f32[8]{0:T(128)S(1)}) all-reduce(f32[8]{0:T(128)S(1)} %get-tuple-element.52, f32[8]{0:T(128)S(1)} %get-tuple-element.51), channel_id=1, replica_groups=mesh['lat'=4,'lon'=8] {'lon'}, use_global_device_ids=true, to_apply=%region_13.15 | all-reduce | flops 16 | bytes 128 | tf_op jit(solution)/shard_map/psum | solution.py:11
  192.1 9.5 %all-reduce.3 = (f32[8]{0:T(128)S(1)}, f32[8]{0:T(128)S(1)}) all-reduce(f32[8]{0:T(128)S(1)} %get-tuple-element.55, f32[8]{0:T(128)S(1)} %get-tuple-element.56), channel_id=1, replica_groups=mesh['lat'=4,'lon'=8] {'lat'}, use_global_device_ids=true, to_apply=%region_14.16 | all-reduce | flops 16 | bytes 128 | tf_op jit(solution)/shard_map/psum | solution.py:12
  201.6 3.7 %multiply_subtract_fusion = (f32[8,192,128]{2,1,0:T(8,128)}, f32[8,192,128]{2,1,0:T(8,128)}) fusion(f32[8,192,128]{2,1,0:T(8,128)} %get-tuple-element.71, f32[8,192,128]{2,1,0:T(8,128)} %get-tuple-element.69, f32[8]{0:T(128)S(1)} %get-tuple-element.68, f32[8]{0:T(128)S(1)} %get-tuple-element.67, f32[8,192,128]{2,1,0:T(8,128)} %get-tuple-element.75, ...), kind=kLoop, calls=%fused_computation.59 | loop fusion | flops 3735552 | bytes 6488224 | tf_op jit(solution)/shard_map/sub | solution.py:91
  (125 shorter events, 28.6 us)
Async XLA Ops:
  0.6 21.4 %copy-start.9 = (s32[192,128]{1,0:T(8,128)S(1)}, s32[192,128]{1,0:T(8,128)}, u32[]{:S(2)}) copy-start(s32[192,128]{1,0:T(8,128)} %param.16) | copy-start | bytes 294916
  0.6 21.4 %copy-start.8 = (f32[192,128]{1,0:T(8,128)S(1)}, f32[192,128]{1,0:T(8,128)}, u32[]{:S(2)}) copy-start(f32[192,128]{1,0:T(8,128)} %param.14) | copy-start | bytes 294916
  0.7 21.4 %copy-start = (f32[8,192,128]{2,1,0:T(8,128)S(1)}, f32[8,192,128]{2,1,0:T(8,128)}, u32[]{:S(2)}) copy-start(f32[8,192,128]{2,1,0:T(8,128)} %param.13) | copy-start | bytes 2359300
  19.0 26.3 %copy-start.7 = (f32[1,192,128]{2,1,0:T(8,128)}, f32[1,192,128]{2,1,0:T(8,128)S(1)}, u32[]{:S(2)}) copy-start(f32[1,192,128]{2,1,0:T(8,128)S(1)} %get-tuple-element.103) | copy-start | bytes 294916
  19.0 6.6 %collective-permute-start.4 = (f32[4,1,128]{2,1,0:T(1,128)S(1)}, f32[4,1,128]{2,1,0:T(1,128)S(1)}, u32[]{:S(2)}, u32[]{:S(2)}) collective-permute-start(f32[4,1,128]{2,1,0:T(1,128)S(1)} %get-tuple-element.105), channel_id=1, source_target_pairs={{0,8},{8,16},{16,24},{24,0},{1,9},{9,17},{17,25},{25,1},{2,10},{10... | collective-permute-start | bytes 6152 | tf_op jit(solution)/shard_map/ppermute | solution.py:26
  20.6 5.0 %collective-permute-start.5 = (f32[4,1,128]{2,1,0:T(1,128)S(1)}, f32[4,1,128]{2,1,0:T(1,128)S(1)}, u32[]{:S(2)}, u32[]{:S(2)}) collective-permute-start(f32[4,1,128]{2,1,0:T(1,128)S(1)} %get-tuple-element.106), channel_id=1, source_target_pairs={{8,0},{16,8},{24,16},{0,24},{9,1},{17,9},{25,17},{1,25},{10,2},{18... | collective-permute-start | bytes 6152 | tf_op jit(solution)/shard_map/ppermute | solution.py:28
  24.7 23.4 %collective-permute-start.1 = (f32[8,192,1]{1,0,2:T(8,128)S(1)}, f32[8,192,1]{1,0,2:T(8,128)S(1)}, u32[]{:S(2)}, u32[]{:S(2)}) collective-permute-start(f32[8,192,1]{1,0,2:T(8,128)S(1)} %copy.91), channel_id=1, source_target_pairs={{1,0},{2,1},{3,2},{4,3},{5,4},{6,5},{7,6},{0,7},{9,8},{10,9},{11,1... | collective-permute-start | bytes 18440 | tf_op jit(solution)/shard_map/ppermute | solution.py:28
  25.1 22.6 %collective-permute-start = (f32[8,192,1]{1,0,2:T(8,128)S(1)}, f32[8,192,1]{1,0,2:T(8,128)S(1)}, u32[]{:S(2)}, u32[]{:S(2)}) collective-permute-start(f32[8,192,1]{1,0,2:T(8,128)S(1)} %copy.90), channel_id=1, source_target_pairs={{0,1},{1,2},{2,3},{3,4},{4,5},{5,6},{6,7},{7,0},{8,9},{9,10},{10,1... | collective-permute-start | bytes 18440 | tf_op jit(solution)/shard_map/ppermute | solution.py:26
  26.7 18.7 %collective-permute-start.6 = (f32[4,194,1]{2,1,0:T(8,128)}, f32[4,194,1]{2,1,0:T(8,128)S(1)}, u32[]{:S(2)}, u32[]{:S(2)}) collective-permute-start(f32[4,194,1]{2,1,0:T(8,128)} %get-tuple-element.99), channel_id=1, source_target_pairs={{0,1},{1,2},{2,3},{3,4},{4,5},{5,6},{6,7},{7,0},{8,9},{9,10},{10,1... | collective-permute-start | bytes 9320 | tf_op jit(solution)/shard_map/ppermute | solution.py:26
  27.7 17.6 %collective-permute-start.7 = (f32[4,194,1]{2,1,0:T(8,128)}, f32[4,194,1]{2,1,0:T(8,128)}, u32[]{:S(2)}, u32[]{:S(2)}) collective-permute-start(f32[4,194,1]{2,1,0:T(8,128)} %get-tuple-element.100), channel_id=1, source_target_pairs={{1,0},{2,1},{3,2},{4,3},{5,4},{6,5},{7,6},{0,7},{9,8},{10,9},{11,1... | collective-permute-start | bytes 9320 | tf_op jit(solution)/shard_map/ppermute | solution.py:28
  48.5 5.7 %collective-permute-start.2 = (f32[8,1,130]{2,0,1:T(8,128)S(1)}, f32[8,1,130]{2,0,1:T(8,128)S(1)}, u32[]{:S(2)}, u32[]{:S(2)}) collective-permute-start(f32[8,1,130]{2,0,1:T(8,128)S(1)} %get-tuple-element.85), channel_id=1, source_target_pairs={{0,8},{8,16},{16,24},{1,9},{9,17},{17,25},{2,10},{10,18},{18,26},{... | collective-permute-start | bytes 12488 | tf_op jit(solution)/shard_map/ppermute | solution.py:26
  51.0 5.9 %collective-permute-start.3 = (f32[8,1,130]{2,0,1:T(8,128)S(1)}, f32[8,1,130]{2,0,1:T(8,128)S(1)}, u32[]{:S(2)}, u32[]{:S(2)}) collective-permute-start(f32[8,1,130]{2,0,1:T(8,128)S(1)} %get-tuple-element.86), channel_id=1, source_target_pairs={{8,0},{16,8},{24,16},{9,1},{17,9},{25,17},{10,2},{18,10},{26,18},{... | collective-permute-start | bytes 12488 | tf_op jit(solution)/shard_map/ppermute | solution.py:28
  62.0 26.0 %copy-start.1 = (f32[8,192,128]{2,1,0:T(8,128)}, f32[8,192,128]{2,1,0:T(8,128)S(1)}, u32[]{:S(2)}) copy-start(f32[8,192,128]{2,1,0:T(8,128)S(1)} %get-tuple-element.78) | copy-start | bytes 2359300
  88.7 4.9 %collective-permute-start.8 = (f32[8,192,1]{1,0,2:T(8,128)S(1)}, f32[8,192,1]{1,0,2:T(8,128)S(1)}, u32[]{:S(2)}, u32[]{:S(2)}) collective-permute-start(f32[8,192,1]{1,0,2:T(8,128)S(1)} %copy.99), channel_id=1, source_target_pairs={{0,1},{1,2},{2,3},{3,4},{4,5},{5,6},{6,7},{7,0},{8,9},{9,10},{10,1... | collective-permute-start | bytes 18440 | tf_op jit(solution)/shard_map/ppermute | solution.py:26
  89.1 4.9 %collective-permute-start.9 = (f32[8,192,1]{1,0,2:T(8,128)S(1)}, f32[8,192,1]{1,0,2:T(8,128)S(1)}, u32[]{:S(2)}, u32[]{:S(2)}) collective-permute-start(f32[8,192,1]{1,0,2:T(8,128)S(1)} %copy.100), channel_id=1, source_target_pairs={{1,0},{2,1},{3,2},{4,3},{5,4},{6,5},{7,6},{0,7},{9,8},{10,9},{11,1... | collective-permute-start | bytes 18440 | tf_op jit(solution)/shard_map/ppermute | solution.py:28
  93.9 17.1 %copy-start.4 = (f32[8,192,1]{2,1,0:T(8,128)}, f32[8,192,1]{2,1,0:T(8,128)S(1)}, u32[]{:S(2)}) copy-start(f32[8,192,1]{2,1,0:T(8,128)S(1)} %copy.101) | copy-start | bytes 18436
  94.3 18.5 %copy-start.6 = (f32[8,192,1]{2,1,0:T(8,128)}, f32[8,192,1]{2,1,0:T(8,128)S(1)}, u32[]{:S(2)}) copy-start(f32[8,192,1]{2,1,0:T(8,128)S(1)} %copy.102) | copy-start | bytes 18436
  94.5 18.3 %collective-permute-start.11 = (f32[8,1,130]{2,0,1:T(8,128)S(1)}, f32[8,1,130]{2,0,1:T(8,128)S(1)}, u32[]{:S(2)}, u32[]{:S(2)}) collective-permute-start(f32[8,1,130]{2,0,1:T(8,128)S(1)} %copy.123), channel_id=1, source_target_pairs={{8,0},{16,8},{24,16},{9,1},{17,9},{25,17},{10,2},{18,10},{26,18},{... | collective-permute-start | bytes 12488 | tf_op jit(solution)/shard_map/ppermute | solution.py:28
  95.8 17.0 %collective-permute-start.10 = (f32[8,1,130]{2,0,1:T(8,128)S(1)}, f32[8,1,130]{2,0,1:T(8,128)S(1)}, u32[]{:S(2)}, u32[]{:S(2)}) collective-permute-start(f32[8,1,130]{2,0,1:T(8,128)S(1)} %copy.103), channel_id=1, source_target_pairs={{0,8},{8,16},{16,24},{1,9},{9,17},{17,25},{2,10},{10,18},{18,26},{... | collective-permute-start | bytes 12488 | tf_op jit(solution)/shard_map/ppermute | solution.py:26
  116.3 26.3 %copy-start.18 = (f32[8]{0:T(128)S(1)}, f32[8]{0:T(128)}, u32[]{:S(2)}) copy-start(f32[8]{0:T(128)} %copy-done.17) | copy-start | bytes 100
  116.3 26.3 %copy-start.20 = (f32[8]{0:T(128)S(1)}, f32[8]{0:T(128)}, u32[]{:S(2)}) copy-start(f32[8]{0:T(128)} %copy-done.19) | copy-start | bytes 100
  146.6 4.9 %collective-permute-start.12 = (f32[8,192,1]{1,0,2:T(8,128)S(1)}, f32[8,192,1]{1,0,2:T(8,128)S(1)}, u32[]{:S(2)}, u32[]{:S(2)}) collective-permute-start(f32[8,192,1]{1,0,2:T(8,128)S(1)} %copy.109), channel_id=1, source_target_pairs={{0,1},{1,2},{2,3},{3,4},{4,5},{5,6},{6,7},{7,0},{8,9},{9,10},{10,1... | collective-permute-start | bytes 18440 | tf_op jit(solution)/shard_map/ppermute | solution.py:26
  147.0 4.9 %collective-permute-start.13 = (f32[8,192,1]{1,0,2:T(8,128)S(1)}, f32[8,192,1]{1,0,2:T(8,128)S(1)}, u32[]{:S(2)}, u32[]{:S(2)}) collective-permute-start(f32[8,192,1]{1,0,2:T(8,128)S(1)} %copy.110), channel_id=1, source_target_pairs={{1,0},{2,1},{3,2},{4,3},{5,4},{6,5},{7,6},{0,7},{9,8},{10,9},{11,1... | collective-permute-start | bytes 18440 | tf_op jit(solution)/shard_map/ppermute | solution.py:28
  151.8 17.1 %copy-start.3 = (f32[8,192,1]{2,1,0:T(8,128)}, f32[8,192,1]{2,1,0:T(8,128)S(1)}, u32[]{:S(2)}) copy-start(f32[8,192,1]{2,1,0:T(8,128)S(1)} %copy.111) | copy-start | bytes 18436
  152.2 18.5 %copy-start.5 = (f32[8,192,1]{2,1,0:T(8,128)}, f32[8,192,1]{2,1,0:T(8,128)S(1)}, u32[]{:S(2)}) copy-start(f32[8,192,1]{2,1,0:T(8,128)S(1)} %copy.112) | copy-start | bytes 18436
  152.4 18.3 %collective-permute-start.15 = (f32[8,1,130]{2,0,1:T(8,128)S(1)}, f32[8,1,130]{2,0,1:T(8,128)S(1)}, u32[]{:S(2)}, u32[]{:S(2)}) collective-permute-start(f32[8,1,130]{2,0,1:T(8,128)S(1)} %copy.124), channel_id=1, source_target_pairs={{8,0},{16,8},{24,16},{9,1},{17,9},{25,17},{10,2},{18,10},{26,18},{... | collective-permute-start | bytes 12488 | tf_op jit(solution)/shard_map/ppermute | solution.py:28
  153.7 17.0 %collective-permute-start.14 = (f32[8,1,130]{2,0,1:T(8,128)S(1)}, f32[8,1,130]{2,0,1:T(8,128)S(1)}, u32[]{:S(2)}, u32[]{:S(2)}) collective-permute-start(f32[8,1,130]{2,0,1:T(8,128)S(1)} %copy.113), channel_id=1, source_target_pairs={{0,8},{8,16},{16,24},{1,9},{9,17},{17,25},{2,10},{10,18},{18,26},{... | collective-permute-start | bytes 12488 | tf_op jit(solution)/shard_map/ppermute | solution.py:26
  174.2 27.4 %copy-start.13 = (f32[8]{0:T(128)S(1)}, f32[8]{0:T(128)}, u32[]{:S(2)}) copy-start(f32[8]{0:T(128)} %copy-done.12) | copy-start | bytes 100
  174.2 27.4 %copy-start.14 = (f32[8]{0:T(128)S(1)}, f32[8]{0:T(128)}, u32[]{:S(2)}) copy-start(f32[8]{0:T(128)} %get-tuple-element.73) | copy-start | bytes 100
  174.2 27.4 %copy-start.2 = (f32[8,192,128]{2,1,0:T(8,128)S(1)}, f32[8,192,128]{2,1,0:T(8,128)}, u32[]{:S(2)}) copy-start(f32[8,192,128]{2,1,0:T(8,128)} %copy-done.1) | copy-start | bytes 2359300
  174.2 27.4 %copy-start.11 = (f32[8]{0:T(128)S(1)}, f32[8]{0:T(128)}, u32[]{:S(2)}) copy-start(f32[8]{0:T(128)} %copy-done.10) | copy-start | bytes 100
  174.3 27.4 %copy-start.16 = (f32[8]{0:T(128)S(1)}, f32[8]{0:T(128)}, u32[]{:S(2)}) copy-start(f32[8]{0:T(128)} %copy-done.15) | copy-start | bytes 100
  (5 other events, 12.4 us)
